TPU v7x, 32 devices: a whole 2x2x4 slice. The times are simulated.
32 devices in a mesh: unit: 1, dp: 16 (over z, y, x), ens: 2 (over core).
Axes of the slice: x: 2, y: 2, z: 4, core: 2. Of those that a mesh axis runs over, the one named last changes fastest.
Arguments:
- samples_in: bfloat16 [4096, 4096], P(('unit', 'dp'), 'ens'), may hold values from -3 to 3, as said below
- second_samples_in: bfloat16 [4096, 4096], P(('unit', 'dp'), 'ens'), may hold values from -3 to 3, as said below
Outputs:
- scaled: float32 [4096, 4096], P('unit', ('ens', 'dp'))
- second_scaled: float32 [4096, 4096], P('unit', ('ens', 'dp'))
Inputs may be any that keep to these rules, and one draw needn't show every extreme that they name: samples_in holds numbers from -3 to 3. second_samples_in holds numbers from -3 to 3.
All inputs are finite; a program needn't handle non-finite values.
Results may differ from a plain program's by a relative error of at most 0.00035.
Values may be sent and summed in bfloat16 or wider, within the bound.
A program may use at most 128 MiB of HBM per device.

v0:
```python
import jax
import jax.numpy as jnp
from jax import lax
from jax.sharding import PartitionSpec as P


def per_device(samples_in, second_samples_in):
    moved_samples_in, moved_second_samples_in = (
        lax.all_to_all(samples_in, "dp", split_axis=1, concat_axis=0, tiled=True),
        lax.all_to_all(second_samples_in, "dp", split_axis=1, concat_axis=0, tiled=True),
    )
    wide_scaled = moved_samples_in.astype(jnp.float32)
    power_scaled = jnp.exp(wide_scaled)
    sum_scaled = jnp.sum(power_scaled, axis=0)
    scaled = power_scaled / sum_scaled * moved_samples_in.shape[0]
    wide_second_scaled = moved_second_samples_in.astype(jnp.float32)
    power_second_scaled = jnp.exp(wide_second_scaled)
    sum_second_scaled = jnp.sum(power_second_scaled, axis=0)
    second_scaled = power_second_scaled / sum_second_scaled * moved_second_samples_in.shape[0]
    return (scaled, second_scaled)


def solution(mesh):
    placed = (P(("unit", "dp"), "ens"), P(("unit", "dp"), "ens"))
    return jax.shard_map(
        per_device,
        mesh=mesh,
        in_specs=placed,
        out_specs=(P("unit", ("ens", "dp")), P("unit", ("ens", "dp"))),
        check_vma=False,
    )
```

profile of v0, /device:TPU:8, one launch (start us, length us, event | category | flops | bytes accessed | tf_op | source)
XLA Modules:
  0.0 66.8 jit_solution(8155692977923089948)
XLA Ops:
  0.6 0.0 copy-start
  0.6 1.2 %copy-done = bf16[256,2048]{1,0:T(8,128)(2,1)S(1)} copy-done((bf16[256,2048]{1,0:T(8,128)(2,1)S(1)}, bf16[256,2048]{1,0:T(8,128)(2,1)}, u32[]{:S(2)}) %copy-start) | copy-done | bytes 1048600
  1.9 0.0 copy-start.1
  1.9 1.2 %copy_bitcast_fusion = bf16[256,16,128]{2,0,1:T(8,128)(2,1)} fusion(bf16[256,2048]{1,0:T(8,128)(2,1)S(1)} %copy-done), kind=kLoop, calls=%fused_computation.6 | loop fusion | bytes 2097152 | tf_op jit(solution)/shard_map/all_to_all | solution.py:10
  3.1 7.2 %all-to-all-start.1 = ((bf16[256,16,128]{2,0,1:T(8,128)(2,1)}), bf16[256,16,128]{2,0,1:T(8,128)(2,1)S(1)}, u32[]{:S(2)}, u32[]{:S(2)}) async-start(bf16[256,16,128]{2,0,1:T(8,128)(2,1)} %copy_bitcast_fusion), calls=%async_computation.1 | async-start | bytes 2097152 | tf_op jit(solution)/shard_map/all_to_all | solution.py:10
  10.3 0.0 copy-done.1
  10.3 1.2 %copy_bitcast_fusion.1 = bf16[256,16,128]{2,0,1:T(8,128)(2,1)} fusion(bf16[256,2048]{1,0:T(8,128)(2,1)S(1)} %copy-done.1), kind=kLoop, calls=%fused_computation.7 | loop fusion | bytes 2097152 | tf_op jit(solution)/shard_map/all_to_all | solution.py:9
  11.6 24.3 %all-to-all-done.1 = bf16[256,16,128]{2,0,1:T(8,128)(2,1)S(1)} async-done(((bf16[256,16,128]{2,0,1:T(8,128)(2,1)}), bf16[256,16,128]{2,0,1:T(8,128)(2,1)S(1)}, u32[]{:S(2)}, u32[]{:S(2)}) %all-to-all-start.1) | async-done | bytes 1048608 | tf_op jit(solution)/shard_map/all_to_all | solution.py:10
  35.9 4.7 %all-to-all-start = ((bf16[256,16,128]{2,0,1:T(8,128)(2,1)}), bf16[256,16,128]{2,0,1:T(8,128)(2,1)S(1)}, u32[]{:S(2)}, u32[]{:S(2)}) async-start(bf16[256,16,128]{2,0,1:T(8,128)(2,1)} %copy_bitcast_fusion.1), calls=%async_computation | async-start | bytes 2097152 | tf_op jit(solution)/shard_map/all_to_all | solution.py:9
  40.6 0.6 fusion.3
  41.2 1.5 %fusion = f32[4096,128]{1,0:T(8,128)} fusion(f32[256,16,128]{2,0,1:T(8,128)S(1)} %get-tuple-element.3, f32[128]{0:T(128)S(1)} %get-tuple-element.2), kind=kLoop, calls=%fused_computation.1 | loop fusion | flops 1048576 | bytes 4194816 | tf_op jit(solution)/shard_map/mul | solution.py:19
  42.6 22.1 %all-to-all-done = bf16[256,16,128]{2,0,1:T(8,128)(2,1)S(1)} async-done(((bf16[256,16,128]{2,0,1:T(8,128)(2,1)}), bf16[256,16,128]{2,0,1:T(8,128)(2,1)S(1)}, u32[]{:S(2)}, u32[]{:S(2)}) %all-to-all-start) | async-done | bytes 1048608 | tf_op jit(solution)/shard_map/all_to_all | solution.py:9
  64.7 0.6 fusion.2
  65.3 1.5 %fusion.1 = f32[4096,128]{1,0:T(8,128)} fusion(f32[256,16,128]{2,0,1:T(8,128)S(1)} %get-tuple-element.5, f32[128]{0:T(128)S(1)} %get-tuple-element.4), kind=kLoop, calls=%fused_computation.3 | loop fusion | flops 1048576 | bytes 4194816 | tf_op jit(solution)/shard_map/mul | solution.py:15
Async XLA Ops:
  0.6 1.2 %copy-start = (bf16[256,2048]{1,0:T(8,128)(2,1)S(1)}, bf16[256,2048]{1,0:T(8,128)(2,1)}, u32[]{:S(2)}) copy-start(bf16[256,2048]{1,0:T(8,128)(2,1)} %param.3) | copy-start | bytes 3145732
  1.9 8.5 %copy-start.1 = (bf16[256,2048]{1,0:T(8,128)(2,1)S(1)}, bf16[256,2048]{1,0:T(8,128)(2,1)}, u32[]{:S(2)}) copy-start(bf16[256,2048]{1,0:T(8,128)(2,1)} %param.2) | copy-start | bytes 3145732
  3.1 32.8 %all-to-all-start.1 = ((bf16[256,16,128]{2,0,1:T(8,128)(2,1)}), bf16[256,16,128]{2,0,1:T(8,128)(2,1)S(1)}, u32[]{:S(2)}, u32[]{:S(2)}) async-start(bf16[256,16,128]{2,0,1:T(8,128)(2,1)} %copy_bitcast_fusion), calls=%async_computation.1 | async-start | bytes 2097152 | tf_op jit(solution)/shard_map/all_to_all | solution.py:10
  35.9 28.9 %all-to-all-start = ((bf16[256,16,128]{2,0,1:T(8,128)(2,1)}), bf16[256,16,128]{2,0,1:T(8,128)(2,1)S(1)}, u32[]{:S(2)}, u32[]{:S(2)}) async-start(bf16[256,16,128]{2,0,1:T(8,128)(2,1)} %copy_bitcast_fusion.1), calls=%async_computation | async-start | bytes 2097152 | tf_op jit(solution)/shard_map/all_to_all | solution.py:9
where the time goes:
time: 67.1 us; the launch traced here: 66.8 us
  waiting for transfers between devices  46.4 us (69%)
  starting transfers between devices  12 us (18%)
  other arithmetic  4.06 us (6%)
  local copies, waits for them, and re-layouts  3.71 us (6%)
    all_to_all x1, waiting for transfers between devices, per_device(): lax.all_to_all(second_samples_in, 'dp', split_axis=1, concat_axis=0, tile...  24.3 us
    all_to_all x1, waiting for transfers between devices, per_device(): lax.all_to_all(samples_in, 'dp', split_axis=1, concat_axis=0, tiled=True)  22.1 us
    all_to_all x1, starting transfers between devices, per_device(): lax.all_to_all(second_samples_in, 'dp', split_axis=1, concat_axis=0, tile...  7.22 us
    all_to_all x1, starting transfers between devices, per_device(): lax.all_to_all(samples_in, 'dp', split_axis=1, concat_axis=0, tiled=True)  4.73 us
    mul x1, other arithmetic, per_device(): scaled = power_scaled / sum_scaled * moved_samples_in.shape[0]  1.47 us
    mul x1, other arithmetic, per_device(): power_second_scaled / sum_second_scaled * moved_second_samples_in.shape[0]  1.47 us
  transfers between devices with their start and end apart: 2, of which 2 were waited for; matrix products, arithmetic and copies ran while one was open for 5% of the time, Pallas kernels for 0%

commit v1 on v0

--- a/solution.py
+++ b/solution.py
@@ -7,7 +7,12 @@
 def per_device(samples_in, second_samples_in):
     moved_samples_in, moved_second_samples_in = (
         lax.all_to_all(samples_in, "dp", split_axis=1, concat_axis=0, tiled=True),
-        lax.all_to_all(second_samples_in, "dp", split_axis=1, concat_axis=0, tiled=True),
+        jnp.concatenate(
+            lax.all_to_all(
+                jnp.stack(jnp.split(second_samples_in, lax.axis_size("dp"), axis=1)), "dp", 0, 0
+            ),
+            axis=0,
+        ),
     )
     wide_scaled = moved_samples_in.astype(jnp.float32)
     power_scaled = jnp.exp(wide_scaled)

time: 67.1 us -> 88.9 us (1.32)
  local copies, waits for them, and re-layouts: 3.71 us -> 24.9 us
    unnamed x4 -> x17, local copies, waits for them, and re-layouts: 1.23 us -> 22.2 us
    another operation x0 -> x1, local copies, waits for them, and re-layouts: none -> 1.47 us  [per_device(): jnp.stack(jnp.split(second_samples_in, lax.axis_size('dp'), axis=1))]
    all_to_all x1 -> x0, local copies, waits for them, and re-layouts: 1.24 us -> none  [per_device(): lax.all_to_all(second_samples_in, 'dp', split_axis=1, concat_axis=0, tile...]
  transfers between devices with their start and end apart: 2 -> 2, of which waited for: 2 -> 2; matrix products, arithmetic and copies ran while one was open for 5% -> 4% of each run, Pallas kernels for 0% -> 0%
where the time goes in v1:
time: 88.9 us; the launch traced here: 88 us
  waiting for transfers between devices  46.4 us (52%)
  local copies, waits for them, and re-layouts  24.9 us (28%)
  starting transfers between devices  12 us (13%)
  other arithmetic  4.06 us (5%)
    all_to_all x1, waiting for transfers between devices, per_device(): lax.all_to_all(jnp.stack(jnp.split(second_samples_in, lax.axis_size('dp')...  24.3 us
    unnamed x17, local copies, waits for them, and re-layouts  22.2 us
    all_to_all x1, waiting for transfers between devices, per_device(): lax.all_to_all(samples_in, 'dp', split_axis=1, concat_axis=0, tiled=True)  22.1 us
    all_to_all x1, starting transfers between devices, per_device(): lax.all_to_all(jnp.stack(jnp.split(second_samples_in, lax.axis_size('dp')...  7.22 us
    all_to_all x1, starting transfers between devices, per_device(): lax.all_to_all(samples_in, 'dp', split_axis=1, concat_axis=0, tiled=True)  4.73 us
  transfers between devices with their start and end apart: 2, of which 2 were waited for; matrix products, arithmetic and copies ran while one was open for 4% of the time, Pallas kernels for 0%

profile of v1, /device:TPU:8, one launch (start us, length us, event | category | flops | bytes accessed | tf_op | source)
XLA Modules:
  0.0 88.0 jit_solution(858223437862864179)
XLA Ops:
  0.6 0.0 copy-start
  0.6 1.6 %bitcast_dynamic-update-slice_fusion.15 = bf16[16,256,128]{2,1,0:T(8,128)(2,1)} fusion(bf16[256,2048]{1,0:T(8,128)(2,1)} %param.3), kind=kLoop, calls=%fused_computation.24 | loop fusion | bytes 131072
  2.2 1.5 %bitcast_dynamic-update-slice_fusion.14 = bf16[16,256,128]{2,1,0:T(8,128)(2,1)} fusion(bf16[16,256,128]{2,1,0:T(8,128)(2,1)} %bitcast_dynamic-update-slice_fusion.15, bf16[256,2048]{1,0:T(8,128)(2,1)} %param.3), kind=kLoop, calls=%fused_computation.23 | loop fusion | bytes 131072
  3.7 1.5 %bitcast_dynamic-update-slice_fusion.13 = bf16[16,256,128]{2,1,0:T(8,128)(2,1)} fusion(bf16[16,256,128]{2,1,0:T(8,128)(2,1)} %bitcast_dynamic-update-slice_fusion.14, bf16[256,2048]{1,0:T(8,128)(2,1)} %param.3), kind=kLoop, calls=%fused_computation.22 | loop fusion | bytes 131072
  5.2 1.5 %bitcast_dynamic-update-slice_fusion.12 = bf16[16,256,128]{2,1,0:T(8,128)(2,1)} fusion(bf16[16,256,128]{2,1,0:T(8,128)(2,1)} %bitcast_dynamic-update-slice_fusion.13, bf16[256,2048]{1,0:T(8,128)(2,1)} %param.3), kind=kLoop, calls=%fused_computation.21 | loop fusion | bytes 131072
  6.6 1.5 %bitcast_dynamic-update-slice_fusion.11 = bf16[16,256,128]{2,1,0:T(8,128)(2,1)} fusion(bf16[16,256,128]{2,1,0:T(8,128)(2,1)} %bitcast_dynamic-update-slice_fusion.12, bf16[256,2048]{1,0:T(8,128)(2,1)} %param.3), kind=kLoop, calls=%fused_computation.20 | loop fusion | bytes 131072
  8.1 1.5 %bitcast_dynamic-update-slice_fusion.10 = bf16[16,256,128]{2,1,0:T(8,128)(2,1)} fusion(bf16[16,256,128]{2,1,0:T(8,128)(2,1)} %bitcast_dynamic-update-slice_fusion.11, bf16[256,2048]{1,0:T(8,128)(2,1)} %param.3), kind=kLoop, calls=%fused_computation.19 | loop fusion | bytes 131072
  9.6 1.5 %bitcast_dynamic-update-slice_fusion.9 = bf16[16,256,128]{2,1,0:T(8,128)(2,1)} fusion(bf16[16,256,128]{2,1,0:T(8,128)(2,1)} %bitcast_dynamic-update-slice_fusion.10, bf16[256,2048]{1,0:T(8,128)(2,1)} %param.3), kind=kLoop, calls=%fused_computation.18 | loop fusion | bytes 131072
  11.0 1.5 %bitcast_dynamic-update-slice_fusion.8 = bf16[16,256,128]{2,1,0:T(8,128)(2,1)} fusion(bf16[16,256,128]{2,1,0:T(8,128)(2,1)} %bitcast_dynamic-update-slice_fusion.9, bf16[256,2048]{1,0:T(8,128)(2,1)} %param.3), kind=kLoop, calls=%fused_computation.17 | loop fusion | bytes 131072
  12.5 1.5 %bitcast_dynamic-update-slice_fusion.7 = bf16[16,256,128]{2,1,0:T(8,128)(2,1)} fusion(bf16[16,256,128]{2,1,0:T(8,128)(2,1)} %bitcast_dynamic-update-slice_fusion.8, bf16[256,2048]{1,0:T(8,128)(2,1)} %param.3), kind=kLoop, calls=%fused_computation.16 | loop fusion | bytes 131072
  14.0 1.5 %bitcast_dynamic-update-slice_fusion.6 = bf16[16,256,128]{2,1,0:T(8,128)(2,1)} fusion(bf16[16,256,128]{2,1,0:T(8,128)(2,1)} %bitcast_dynamic-update-slice_fusion.7, bf16[256,2048]{1,0:T(8,128)(2,1)} %param.3), kind=kLoop, calls=%fused_computation.15 | loop fusion | bytes 131072
  15.5 1.5 %bitcast_dynamic-update-slice_fusion.5 = bf16[16,256,128]{2,1,0:T(8,128)(2,1)} fusion(bf16[16,256,128]{2,1,0:T(8,128)(2,1)} %bitcast_dynamic-update-slice_fusion.6, bf16[256,2048]{1,0:T(8,128)(2,1)} %param.3), kind=kLoop, calls=%fused_computation.14 | loop fusion | bytes 131072
  16.9 1.5 %bitcast_dynamic-update-slice_fusion.4 = bf16[16,256,128]{2,1,0:T(8,128)(2,1)} fusion(bf16[16,256,128]{2,1,0:T(8,128)(2,1)} %bitcast_dynamic-update-slice_fusion.5, bf16[256,2048]{1,0:T(8,128)(2,1)} %param.3), kind=kLoop, calls=%fused_computation.13 | loop fusion | bytes 131072
  18.4 1.5 %bitcast_dynamic-update-slice_fusion.3 = bf16[16,256,128]{2,1,0:T(8,128)(2,1)} fusion(bf16[16,256,128]{2,1,0:T(8,128)(2,1)} %bitcast_dynamic-update-slice_fusion.4, bf16[256,2048]{1,0:T(8,128)(2,1)} %param.3), kind=kLoop, calls=%fused_computation.12 | loop fusion | bytes 131072
  19.9 1.5 %bitcast_dynamic-update-slice_fusion.2 = bf16[16,256,128]{2,1,0:T(8,128)(2,1)} fusion(bf16[16,256,128]{2,1,0:T(8,128)(2,1)} %bitcast_dynamic-update-slice_fusion.3, bf16[256,2048]{1,0:T(8,128)(2,1)} %param.3), kind=kLoop, calls=%fused_computation.11 | loop fusion | bytes 131072
  21.4 1.5 %bitcast_dynamic-update-slice_fusion.1 = bf16[16,256,128]{2,1,0:T(8,128)(2,1)} fusion(bf16[16,256,128]{2,1,0:T(8,128)(2,1)} %bitcast_dynamic-update-slice_fusion.2, bf16[256,2048]{1,0:T(8,128)(2,1)} %param.3), kind=kLoop, calls=%fused_computation.10 | loop fusion | bytes 131072
  22.8 1.5 %bitcast_dynamic-update-slice_fusion = bf16[16,256,128]{2,1,0:T(8,128)(2,1)} fusion(bf16[16,256,128]{2,1,0:T(8,128)(2,1)} %bitcast_dynamic-update-slice_fusion.1, bf16[256,2048]{1,0:T(8,128)(2,1)} %param.3), kind=kLoop, calls=%fused_computation.9 | loop fusion | bytes 131072 | tf_op jit(solution)/shard_map/stack | solution.py:12
  24.3 7.2 %all-to-all-start.1 = ((bf16[16,256,128]{2,1,0:T(8,128)(2,1)}), bf16[16,256,128]{2,1,0:T(8,128)(2,1)S(1)}, u32[]{:S(2)}, u32[]{:S(2)}) async-start(bf16[16,256,128]{2,1,0:T(8,128)(2,1)} %bitcast_dynamic-update-slice_fusion), calls=%async_computation.1 | async-start | bytes 2097152 | tf_op jit(solution)/shard_map/all_to_all | solution.py:11
  31.5 0.0 copy-done
  31.5 1.2 %copy_bitcast_fusion = bf16[256,16,128]{2,0,1:T(8,128)(2,1)} fusion(bf16[256,2048]{1,0:T(8,128)(2,1)S(1)} %copy-done), kind=kLoop, calls=%fused_computation.6 | loop fusion | bytes 2097152 | tf_op jit(solution)/shard_map/all_to_all | solution.py:9
  32.8 24.3 %all-to-all-done.1 = bf16[16,256,128]{2,1,0:T(8,128)(2,1)S(1)} async-done(((bf16[16,256,128]{2,1,0:T(8,128)(2,1)}), bf16[16,256,128]{2,1,0:T(8,128)(2,1)S(1)}, u32[]{:S(2)}, u32[]{:S(2)}) %all-to-all-start.1) | async-done | bytes 1048608 | tf_op jit(solution)/shard_map/all_to_all | solution.py:11
  57.1 4.7 %all-to-all-start = ((bf16[256,16,128]{2,0,1:T(8,128)(2,1)}), bf16[256,16,128]{2,0,1:T(8,128)(2,1)S(1)}, u32[]{:S(2)}, u32[]{:S(2)}) async-start(bf16[256,16,128]{2,0,1:T(8,128)(2,1)} %copy_bitcast_fusion), calls=%async_computation | async-start | bytes 2097152 | tf_op jit(solution)/shard_map/all_to_all | solution.py:9
  61.8 0.6 fusion.3
  62.4 1.5 %fusion.1 = f32[4096,128]{1,0:T(8,128)} fusion(f32[16,256,128]{2,1,0:T(8,128)S(1)} %get-tuple-element.3, f32[128]{0:T(128)S(1)} %get-tuple-element.2), kind=kLoop, calls=%fused_computation.3 | loop fusion | flops 1048576 | bytes 4194816 | tf_op jit(solution)/shard_map/mul | solution.py:24
  63.8 22.1 %all-to-all-done = bf16[256,16,128]{2,0,1:T(8,128)(2,1)S(1)} async-done(((bf16[256,16,128]{2,0,1:T(8,128)(2,1)}), bf16[256,16,128]{2,0,1:T(8,128)(2,1)S(1)}, u32[]{:S(2)}, u32[]{:S(2)}) %all-to-all-start) | async-done | bytes 1048608 | tf_op jit(solution)/shard_map/all_to_all | solution.py:9
  85.9 0.6 fusion.2
  86.5 1.5 %fusion = f32[4096,128]{1,0:T(8,128)} fusion(f32[256,16,128]{2,0,1:T(8,128)S(1)} %get-tuple-element.5, f32[128]{0:T(128)S(1)} %get-tuple-element.4), kind=kLoop, calls=%fused_computation.1 | loop fusion | flops 1048576 | bytes 4194816 | tf_op jit(solution)/shard_map/mul | solution.py:20
Async XLA Ops:
  0.6 30.9 %copy-start = (bf16[256,2048]{1,0:T(8,128)(2,1)S(1)}, bf16[256,2048]{1,0:T(8,128)(2,1)}, u32[]{:S(2)}) copy-start(bf16[256,2048]{1,0:T(8,128)(2,1)} %param.2) | copy-start | bytes 3145732
  24.3 32.8 %all-to-all-start.1 = ((bf16[16,256,128]{2,1,0:T(8,128)(2,1)}), bf16[16,256,128]{2,1,0:T(8,128)(2,1)S(1)}, u32[]{:S(2)}, u32[]{:S(2)}) async-start(bf16[16,256,128]{2,1,0:T(8,128)(2,1)} %bitcast_dynamic-update-slice_fusion), calls=%async_computation.1 | async-start | bytes 2097152 | tf_op jit(solution)/shard_map/all_to_all | solution.py:11
  57.1 28.9 %all-to-all-start = ((bf16[256,16,128]{2,0,1:T(8,128)(2,1)}), bf16[256,16,128]{2,0,1:T(8,128)(2,1)S(1)}, u32[]{:S(2)}, u32[]{:S(2)}) async-start(bf16[256,16,128]{2,0,1:T(8,128)(2,1)} %copy_bitcast_fusion), calls=%async_computation | async-start | bytes 2097152 | tf_op jit(solution)/shard_map/all_to_all | solution.py:9
